TPU v7x, 32 devices: a whole 2x2x4 slice. The times are simulated.
32 devices in a mesh: row: 8 (over z, y), col: 4 (over x, core).
Axes of the slice: x: 2, y: 2, z: 4, core: 2. Of those that a mesh axis runs over, the one named last changes fastest.
Arguments:
- tokens: bfloat16 [4096, 4096], P('row', 'col'), may hold values from -6 to 6
- norm_gain: bfloat16 [4096], P('col'), may hold values from 0.099609375 to 1.8984375
- gate_weight: bfloat16 [4096, 10240], P('row', 'col'), may hold values from -0.09375 to 0.09375
- linear_weight: bfloat16 [4096, 10240], P('row', 'col'), may hold values from -0.09375 to 0.09375
- output_weight: bfloat16 [10240, 4096], P('col', 'row'), may hold values from -0.078125 to 0.078125
Outputs:
- block_out: bfloat16 [4096, 4096], P('row', 'col')
All inputs are finite; a program needn't handle non-finite values.
Results may differ from a plain program's by a relative error of at most 0.0065.
Values may be sent and summed in bfloat16 or wider, within the bound.
A program may use at most 128 MiB of HBM per device.

v0:
```python
import jax
import jax.numpy as jnp
from jax import lax
from jax.sharding import PartitionSpec as P


LANES = 128
CHUNKS = 2


def gathered(tokens, norm_gain, gate_weight, linear_weight, output_weight):
    whole = lax.all_gather(tokens, "col", axis=1, tiled=True)
    gain_all = lax.all_gather(norm_gain, "col", axis=0, tiled=True)
    normed = rms_normed(whole, gain_all)
    gate = dot(normed, lax.all_gather(gate_weight, "row", axis=0, tiled=True))
    linear = dot(normed, lax.all_gather(linear_weight, "row", axis=0, tiled=True))
    hidden = (jax.nn.gelu(gate, approximate=True) * linear).astype(jnp.bfloat16)
    terms = dot(hidden, lax.all_gather(output_weight, "row", axis=1, tiled=True))
    return lax.psum_scatter(terms, "col", scatter_dimension=1, tiled=True).astype(jnp.bfloat16)


def dot(left, right):
    return jnp.dot(left, right, preferred_element_type=jnp.float32)


def rms_normed(whole, gain_all):
    values = whole.astype(jnp.float32)
    meansq = jnp.mean(values * values, axis=-1, keepdims=True)
    return (values * lax.rsqrt(meansq + 1e-06) * gain_all.astype(jnp.float32)).astype(jnp.bfloat16)


def added(left, right):
    return (left.astype(jnp.float32) + right.astype(jnp.float32)).astype(jnp.bfloat16)


def spread(zs, ys, xs, cores, tokens, norm_gain, gate_weight, linear_weight, output_weight):
    row, col = lax.axis_index("row"), lax.axis_index("col")
    z, y = row // ys, row % ys
    size, width = tokens.shape
    size_in = gate_weight.shape[0]

    def along_z(value, step, back, ahead):
        pairs = [
            (a * ys + b, (a + step) * ys + b)
            for a in range(zs)
            for b in range(ys)
            if 0 <= a - step * back < zs and 0 <= a + step * ahead < zs
        ]
        return lax.ppermute(value, "row", pairs)

    def round_z(value, step):
        pairs = [(a * ys + b, (a + step) % zs * ys + b) for a in range(zs) for b in range(ys)]
        return lax.ppermute(value, "row", pairs)

    def other_y(value):
        return lax.ppermute(
            value, "row", [(a * ys + b, a * ys + 1 - b) for a in range(zs) for b in range(ys)]
        )

    def other_x(value):
        return lax.ppermute(
            value, "col", [(a * cores + b, (1 - a) * cores + b) for a in range(xs) for b in range(cores)]
        )

    def other_core(value):
        return lax.ppermute(
            value, "col", [(a * cores + b, a * cores + 1 - b) for a in range(xs) for b in range(cores)]
        )

    def to_col(value, other):
        return other(value)

    across = [to_col(tokens, other_x)]
    right, left = [tokens], [tokens]
    for hop in range(zs - 1):
        right.append(along_z(right[-1], 1, hop, 1))
        left.append(along_z(left[-1], -1, hop, 1))
    rest = jnp.concatenate(
        [jnp.where(z >= s, right[s], left[zs - s]) for s in range(1, zs)], axis=0
    )
    across.append(to_col(rest, other_x))
    mine = jnp.concatenate([tokens, rest], axis=0)
    across = jnp.concatenate(across, axis=0)
    mine_pair = to_col(mine, other_core)
    across_pair = to_col(across, other_core)
    whole = jnp.concatenate([mine, mine_pair, across, across_pair], axis=1)
    gains = lax.all_gather(norm_gain, "col", axis=0, tiled=True)
    gain_all = jnp.concatenate(
        [lax.dynamic_slice_in_dim(gains, (col ^ k) * width, width, 0) for k in range(xs * cores)]
    )

    def piece_of(weight, dim, step):
        part = weight.shape[dim] // zs
        return lax.dynamic_slice_in_dim(weight, (z + step) % zs * part, part, dim)

    def both_y(pieces):
        found = []
        for step, piece in enumerate(pieces):
            piece = round_z(piece, step) if step else piece
            passed = other_y(piece)
            found.append(((z - step) % zs * ys + y, piece))
            found.append(((z - step) % zs * ys + 1 - y, passed))
        return found

    depth = size_in
    inputs = both_y(
        [
            jnp.concatenate([piece_of(w, 1, step) for w in (gate_weight, linear_weight)], axis=0)
            for step in range(zs)
        ],
    )
    outputs = both_y([piece_of(output_weight, 0, step) for step in range(zs)])
    part = gate_weight.shape[1] // zs

    gate_all = jnp.zeros((width * xs * cores, part), gate_weight.dtype)
    linear_all, output_all = gate_all, jnp.zeros((part, width * xs * cores), gate_weight.dtype)
    for origin, piece in inputs:
        place = ((origin * depth // width) ^ col) * width + origin * depth % width
        gate_all = lax.dynamic_update_slice_in_dim(gate_all, piece[:depth], place, 0)
        linear_all = lax.dynamic_update_slice_in_dim(linear_all, piece[depth:], place, 0)
    for origin, piece in outputs:
        k = (origin * depth // width) ^ col
        place = ((1 - k % cores) * xs + k // cores) * width + origin * depth % width
        output_all = lax.dynamic_update_slice_in_dim(output_all, piece, place, 1)

    normed = rms_normed(whole, gain_all)
    gate = dot(normed, gate_all)
    linear = dot(normed, linear_all)
    hidden = (jax.nn.gelu(gate, approximate=True) * linear).astype(jnp.bfloat16)
    hidden = hidden.reshape(zs, size, -1)

    rows = size // CHUNKS
    half = xs * width
    outs = []
    for chunk in range(CHUNKS):
        left_rows = hidden[:, chunk * rows : (chunk + 1) * rows].reshape(zs * rows, -1)
        given = dot(left_rows, output_all[:, :half]).astype(jnp.bfloat16)
        came = to_col(given, other_core)
        far_terms = dot(left_rows, output_all[:, half + width :])
        far_terms = added(far_terms, came[:, width:])
        across_terms = to_col(far_terms, other_x)
        terms = dot(left_rows, output_all[:, half : half + width])
        terms = terms + came[:, :width].astype(jnp.float32)
        terms = (terms + across_terms.astype(jnp.float32)).astype(jnp.bfloat16)

        def block(at):
            return lax.dynamic_slice_in_dim(terms, (z - at) % zs * rows, rows, 0)

        total = terms[:rows].astype(jnp.float32)
        for way in (1, -1):
            carried = None
            for far in range(zs - 1, 0, -1):
                send = block(z + way * far)
                if carried is not None:
                    send = added(send, carried)
                carried = along_z(send, way, 0, far)
            total = total + carried.astype(jnp.float32)
        outs.append(total.astype(jnp.bfloat16))
    return jnp.concatenate(outs, axis=0)


def solution(mesh):
    rows, cols = mesh.shape["row"], mesh.shape["col"]
    zs, ys, xs, cores = rows // 2, 2, cols // 2, 2

    def fits(gate_weight):
        return xs == 2 and gate_weight[1] // cols % (zs * LANES) == 0

    def local(tokens, norm_gain, gate_weight, linear_weight, output_weight):
        args = (tokens, norm_gain, gate_weight, linear_weight, output_weight)
        if fits((gate_weight.shape[0], gate_weight.shape[1] * cols)):
            return spread(zs, ys, xs, cores, *args)
        return gathered(*args)

    return jax.shard_map(
        local,
        mesh=mesh,
        in_specs=(P("row", "col"), P("col"), P("row", "col"), P("row", "col"), P("col", "row")),
        out_specs=P("row", "col"),
        check_vma=False,
    )
```

profile of v0, /device:TPU:0, one launch (start us, length us, event | category | flops | bytes accessed | tf_op | source)
XLA Modules:
  0.0 720.7 jit_solution(5035716951362990686)
XLA Ops:
  0.0 5.0 collective-permute-start
  6.3 21.3 %collective-permute-done = bf16[512,1024]{1,0:T(8,128)(2,1)S(1)} collective-permute-done((bf16[512,1024]{1,0:T(8,128)(2,1)}, bf16[512,1024]{1,0:T(8,128)(2,1)S(1)}, u32[]{:S(2)}, u32[]{:S(2)}) %collective-permute-start) | collective-permute-done | bytes 1048608 | tf_op jit(solution)/shard_map/ppermute | solution.py:49
  28.4 3.4 collective-permute-done.1
  34.7 22.9 %collective-permute-done.2 = bf16[512,1024]{1,0:T(8,128)(2,1)} collective-permute-done((bf16[512,1024]{1,0:T(8,128)(2,1)S(1)}, bf16[512,1024]{1,0:T(8,128)(2,1)}, u32[]{:S(2)}, u32[]{:S(2)}) %collective-permute-start.2) | collective-permute-done | bytes 1048608 | tf_op jit(solution)/shard_map/ppermute | solution.py:49
  60.5 22.3 %collective-permute-done.3 = bf16[512,1024]{1,0:T(8,128)(2,1)} collective-permute-done((bf16[512,1024]{1,0:T(8,128)(2,1)}, bf16[512,1024]{1,0:T(8,128)(2,1)}, u32[]{:S(2)}, u32[]{:S(2)}) %collective-permute-start.3) | collective-permute-done | bytes 1048608 | tf_op jit(solution)/shard_map/ppermute | solution.py:49
  88.2 3.1 constant_dynamic-slice_fusion.4
  93.9 82.2 %collective-permute-done.7 = bf16[512,1024]{1,0:T(8,128)(2,1)} collective-permute-done((bf16[512,1024]{1,0:T(8,128)(2,1)}, bf16[512,1024]{1,0:T(8,128)(2,1)}, u32[]{:S(2)}, u32[]{:S(2)}) %collective-permute-start.7) | collective-permute-done | bytes 1048608 | tf_op jit(solution)/shard_map/ppermute | solution.py:61
  178.4 3.4 pad_maximum_fusion.1
  182.5 3.9 constant_dynamic-update-slice_fusion
  187.4 14.9 %collective-permute-done.20 = bf16[640,512]{1,0:T(8,128)(2,1)} collective-permute-done((bf16[640,512]{1,0:T(8,128)(2,1)S(1)}, bf16[640,512]{1,0:T(8,128)(2,1)}, u32[]{:S(2)}, u32[]{:S(2)}) %collective-permute-start.20) | collective-permute-done | bytes 655392 | tf_op jit(solution)/shard_map/ppermute | solution.py:53
  202.3 13.6 %collective-permute-start.11 = (bf16[1024,640]{1,0:T(8,128)(2,1)S(1)}, bf16[1024,640]{1,0:T(8,128)(2,1)}, u32[]{:S(2)}, u32[]{:S(2)}) collective-permute-start(bf16[1024,640]{1,0:T(8,128)(2,1)S(1)} %pad_maximum_fusion.4), channel_id=1, source_target_pairs={{0,8},{4,12},{8,16},{12,20},{16,24},{20,28},{24,0},{28,4},{1,9},{5... | collective-permute-start | bytes 3932168 | tf_op jit(solution)/shard_map/ppermute | solution.py:53
  216.1 3.6 collective-permute-start.13
  219.8 28.9 %collective-permute-done.11 = bf16[1024,640]{1,0:T(8,128)(2,1)} collective-permute-done((bf16[1024,640]{1,0:T(8,128)(2,1)S(1)}, bf16[1024,640]{1,0:T(8,128)(2,1)}, u32[]{:S(2)}, u32[]{:S(2)}) %collective-permute-start.11) | collective-permute-done | bytes 1310752 | tf_op jit(solution)/shard_map/ppermute | solution.py:53
  250.3 53.5 %collective-permute-done.13 = bf16[1024,640]{1,0:T(8,128)(2,1)} collective-permute-done((bf16[1024,640]{1,0:T(8,128)(2,1)S(1)}, bf16[1024,640]{1,0:T(8,128)(2,1)}, u32[]{:S(2)}, u32[]{:S(2)}) %collective-permute-start.13) | collective-permute-done | bytes 1310752 | tf_op jit(solution)/shard_map/ppermute | solution.py:53
  305.8 2.8 broadcast_in_dim.8.clone
  308.6 4.2 dynamic_update_slice.72
  312.8 2.8 broadcast_in_dim.8.clone.1
  315.6 4.2 dynamic_update_slice.80
  319.7 2.9 broadcast_in_dim.9
  322.6 6.9 dynamic_update_slice.88
  329.6 5.2 all_gather.3
  336.3 7.1 dynamic_update_slice.89
  343.4 6.9 dynamic_update_slice.90
  353.3 4.2 dynamic_update_slice.73
  357.4 4.2 dynamic_update_slice.81
  365.6 4.2 dynamic_update_slice.74
  369.7 4.2 dynamic_update_slice.82
  373.9 6.9 dynamic_update_slice.91
  380.8 6.9 dynamic_update_slice.92
  387.7 6.3 dynamic_update_slice.93
  394.0 6.9 dynamic_update_slice.94
  400.9 6.9 dynamic_update_slice.95
  410.3 2.6 fusion.32
  412.9 2.5 fusion.35
  415.4 4.1 dynamic_update_slice.75
  419.5 4.1 dynamic_update_slice.83
  423.7 4.1 dynamic_update_slice.76
  427.8 4.2 dynamic_update_slice.84
  434.4 4.1 dynamic_update_slice.77
  438.6 4.2 dynamic_update_slice.85
  442.7 4.2 dynamic_update_slice.78
  446.9 4.2 dynamic_update_slice.86
  451.1 2.5 fusion.31
  453.6 4.2 dynamic_update_slice.79
  457.7 4.2 dynamic_update_slice.87
  461.9 28.2 %fusion = (f32[2048]{0:T(1024)S(1)}, bf16[2048,4096]{1,0:T(8,128)(2,1)}) fusion(bf16[2048,1024]{1,0:T(8,128)(2,1)} %collective-permute-done.9, bf16[2048,1024]{1,0:T(8,128)(2,1)} %constant_dynamic-update-slice_fusion, bf16[2048,1024]{1,0:T(8,128)(2,1)} %collective-permute-done.6, bf16[512,1024]{1,0:T(8,128)(2,1)S(1)} %broadcast_select_fusion, ...), kind=kLoop, calls=%fused_computation.2 | loop fusion | flops 142604288 | bytes 33562624 | tf_op jit(solution)/shard_map/reduce_sum | solution.py:28
  490.2 19.6 %fusion.14 = f32[2048,640]{1,0:T(8,128)} fusion(bf16[4096,640]{1,0:T(8,128)(2,1)} %dynamic_update_slice.79, bf16[2048,4096]{1,0:T(8,128)(2,1)} %get-tuple-element.6, f32[4096]{0:T(1024)S(1)} %maximum_convert_fusion, f32[2048]{0:T(1024)S(1)} %add_rsqrt_fusion), kind=kOutput, calls=%fused_computation.17 | convolution fusion | flops 10770972672 | bytes 27287552 | tf_op jit(solution)/shard_map/dot_general | solution.py:23
  509.7 17.4 %fusion.11 = bf16[2048,640]{1,0:T(8,128)(2,1)S(1)} fusion(f32[2048,640]{1,0:T(8,128)} %fusion.14, bf16[4096,640]{1,0:T(8,128)(2,1)} %dynamic_update_slice.87, bf16[2048,4096]{1,0:T(8,128)(2,1)S(1)} %copy-done, f32[4096]{0:T(1024)S(1)} %maximum_convert_fusion, f32[2048]{0:T(1024)S(1)} %add_rsqrt_fusion), kind=kOutput, calls=%fused_computation.15 | convolution fusion | flops 10784079872 | bytes 29908992 | tf_op jit(solution)/shard_map/dot_general | solution.py:23
  527.5 3.6 convolution_convert_fusion
  531.2 3.6 convolution_convert_fusion.1
  535.4 2.9 collective-permute-done.32
  541.1 3.3 collective-permute-done.24
  547.1 41.7 %collective-permute-done.33 = bf16[1024,1024]{1,0:T(8,128)(2,1)S(1)} collective-permute-done((bf16[1024,1024]{1,0:T(8,128)(2,1)S(1)}, bf16[1024,1024]{1,0:T(8,128)(2,1)S(1)}, u32[]{:S(2)}, u32[]{:S(2)}) %collective-permute-start.33) | collective-permute-done | bytes 2097184 | tf_op jit(solution)/shard_map/ppermute | solution.py:61
  590.8 29.0 %collective-permute-start.34 = (bf16[256,1024]{1,0:T(8,128)(2,1)S(1)}, bf16[256,1024]{1,0:T(8,128)(2,1)S(1)}, u32[]{:S(2)}, u32[]{:S(2)}) collective-permute-start(bf16[256,1024]{1,0:T(8,128)(2,1)S(1)} %get-tuple-element.31), channel_id=1, source_target_pairs={{0,8},{4,12},{1,9},{5,13},{2,10},{6,14},{3,11},{7,15}} | collective-permute-start | bytes 1572872 | tf_op jit(solution)/shard_map/ppermute | solution.py:49
  620.7 12.1 %collective-permute-done.25 = bf16[1024,1024]{1,0:T(8,128)(2,1)S(1)} collective-permute-done((bf16[1024,1024]{1,0:T(8,128)(2,1)S(1)}, bf16[1024,1024]{1,0:T(8,128)(2,1)S(1)}, u32[]{:S(2)}, u32[]{:S(2)}) %collective-permute-start.25) | collective-permute-done | bytes 2097184 | tf_op jit(solution)/shard_map/ppermute | solution.py:61
  634.9 29.0 %collective-permute-start.26 = (bf16[256,1024]{1,0:T(8,128)(2,1)S(1)}, bf16[256,1024]{1,0:T(8,128)(2,1)S(1)}, u32[]{:S(2)}, u32[]{:S(2)}) collective-permute-start(bf16[256,1024]{1,0:T(8,128)(2,1)S(1)} %get-tuple-element.25), channel_id=1, source_target_pairs={{0,8},{4,12},{1,9},{5,13},{2,10},{6,14},{3,11},{7,15}} | collective-permute-start | bytes 1572872 | tf_op jit(solution)/shard_map/ppermute | solution.py:49
  667.0 9.2 %collective-permute-done.26 = bf16[256,1024]{1,0:T(8,128)(2,1)S(1)} collective-permute-done((bf16[256,1024]{1,0:T(8,128)(2,1)S(1)}, bf16[256,1024]{1,0:T(8,128)(2,1)S(1)}, u32[]{:S(2)}, u32[]{:S(2)}) %collective-permute-start.26) | collective-permute-done | bytes 524320 | tf_op jit(solution)/shard_map/ppermute | solution.py:49
  676.5 4.4 collective-permute-start.27
  681.6 5.8 collective-permute-done.35
  689.1 5.0 collective-permute-start.36
  694.2 4.5 collective-permute-done.27
  700.3 5.0 collective-permute-start.28
  705.4 4.5 collective-permute-done.36
  712.2 7.2 collective-permute-done.28
  (109 shorter events, 59.3 us)
Async XLA Ops:
  0.0 27.7 %collective-permute-start = (bf16[512,1024]{1,0:T(8,128)(2,1)}, bf16[512,1024]{1,0:T(8,128)(2,1)S(1)}, u32[]{:S(2)}, u32[]{:S(2)}) collective-permute-start(bf16[512,1024]{1,0:T(8,128)(2,1)} %param.5), channel_id=1, source_target_pairs={{0,8},{4,12},{8,16},{12,20},{16,24},{20,28},{1,9},{5,13},{9,17},{1... | collective-permute-start | bytes 3145736 | tf_op jit(solution)/shard_map/ppermute | solution.py:49
  5.0 26.7 %collective-permute-start.1 = (bf16[512,1024]{1,0:T(8,128)(2,1)}, bf16[512,1024]{1,0:T(8,128)(2,1)S(1)}, u32[]{:S(2)}, u32[]{:S(2)}) collective-permute-start(bf16[512,1024]{1,0:T(8,128)(2,1)} %param.5), channel_id=1, source_target_pairs={{8,0},{12,4},{16,8},{20,12},{24,16},{28,20},{9,1},{13,5},{17,9},{2... | collective-permute-start | bytes 3145736 | tf_op jit(solution)/shard_map/ppermute | solution.py:49
  27.7 31.3 %copy-start.5 = (bf16[512,1024]{1,0:T(8,128)(2,1)}, bf16[512,1024]{1,0:T(8,128)(2,1)S(1)}, u32[]{:S(2)}) copy-start(bf16[512,1024]{1,0:T(8,128)(2,1)S(1)} %collective-permute-done) | copy-start | bytes 3145732
  27.7 5.4 collective-permute-start.4
  31.7 25.9 %collective-permute-start.2 = (bf16[512,1024]{1,0:T(8,128)(2,1)S(1)}, bf16[512,1024]{1,0:T(8,128)(2,1)}, u32[]{:S(2)}, u32[]{:S(2)}) collective-permute-start(bf16[512,1024]{1,0:T(8,128)(2,1)S(1)} %collective-permute-done.1), channel_id=1, source_target_pairs={{8,0},{12,4},{16,8},{20,12},{9,1},{13,5},{17,9},{21,13},{10,2},{14... | collective-permute-start | bytes 3145736 | tf_op jit(solution)/shard_map/ppermute | solution.py:49
  33.0 27.4 %collective-permute-start.5 = (bf16[512,1024]{1,0:T(8,128)(2,1)S(1)}, bf16[512,1024]{1,0:T(8,128)(2,1)}, u32[]{:S(2)}, u32[]{:S(2)}) collective-permute-start(bf16[512,1024]{1,0:T(8,128)(2,1)S(1)} %collective-permute-done.4), channel_id=1, source_target_pairs={{16,24},{20,28},{17,25},{21,29},{18,26},{22,30},{19,27},{23,31}} | collective-permute-start | bytes 3145736 | tf_op jit(solution)/shard_map/ppermute | solution.py:49
  57.6 25.2 %collective-permute-start.3 = (bf16[512,1024]{1,0:T(8,128)(2,1)}, bf16[512,1024]{1,0:T(8,128)(2,1)}, u32[]{:S(2)}, u32[]{:S(2)}) collective-permute-start(bf16[512,1024]{1,0:T(8,128)(2,1)} %collective-permute-done.2), channel_id=1, source_target_pairs={{8,0},{12,4},{9,1},{13,5},{10,2},{14,6},{11,3},{15,7}} | collective-permute-start | bytes 3145736 | tf_op jit(solution)/shard_map/ppermute | solution.py:49
  59.0 23.9 %copy-start.6 = (bf16[512,1024]{1,0:T(8,128)(2,1)S(1)}, bf16[512,1024]{1,0:T(8,128)(2,1)}, u32[]{:S(2)}) copy-start(bf16[512,1024]{1,0:T(8,128)(2,1)} %copy-done.5) | copy-start | bytes 3145732
  86.2 95.6 %collective-permute-start.8 = (bf16[1536,1024]{1,0:T(8,128)(2,1)}, bf16[1536,1024]{1,0:T(8,128)(2,1)}, u32[]{:S(2)}, u32[]{:S(2)}) collective-permute-start(bf16[1536,1024]{1,0:T(8,128)(2,1)} %pad_maximum_fusion.2), channel_id=1, source_target_pairs={{0,2},{1,3},{2,0},{3,1},{4,6},{5,7},{6,4},{7,5},{8,10},{9,11},{10,... | collective-permute-start | bytes 9437192 | tf_op jit(solution)/shard_map/ppermute | solution.py:61
  87.7 88.4 %collective-permute-start.7 = (bf16[512,1024]{1,0:T(8,128)(2,1)}, bf16[512,1024]{1,0:T(8,128)(2,1)}, u32[]{:S(2)}, u32[]{:S(2)}) collective-permute-start(bf16[512,1024]{1,0:T(8,128)(2,1)} %param.5), channel_id=1, source_target_pairs={{0,2},{1,3},{2,0},{3,1},{4,6},{5,7},{6,4},{7,5},{8,10},{9,11},{10,... | collective-permute-start | bytes 3145736 | tf_op jit(solution)/shard_map/ppermute | solution.py:61
  88.2 4.9 copy-start.3
  91.3 87.1 %copy-start.1 = (bf16[512,640]{1,0:T(8,128)(2,1)}, bf16[512,640]{1,0:T(8,128)(2,1)S(1)}, u32[]{:S(2)}) copy-start(bf16[512,640]{1,0:T(8,128)(2,1)S(1)} %get-tuple-element.19) | copy-start | bytes 1966084
  91.4 87.1 %copy-start.2 = (bf16[512,640]{1,0:T(8,128)(2,1)}, bf16[512,640]{1,0:T(8,128)(2,1)S(1)}, u32[]{:S(2)}) copy-start(bf16[512,640]{1,0:T(8,128)(2,1)S(1)} %get-tuple-element.52) | copy-start | bytes 1966084
  91.5 128.3 %collective-permute-start.10 = (bf16[1024,640]{1,0:T(8,128)(2,1)S(1)}, bf16[1024,640]{1,0:T(8,128)(2,1)}, u32[]{:S(2)}, u32[]{:S(2)}) collective-permute-start(bf16[1024,640]{1,0:T(8,128)(2,1)S(1)} %pad_maximum_fusion.3), channel_id=1, source_target_pairs={{0,4},{4,0},{8,12},{12,8},{16,20},{20,16},{24,28},{28,24},{1,5},{5... | collective-permute-start | bytes 3932168 | tf_op jit(solution)/shard_map/ppermute | solution.py:56
  93.3 88.4 %copy-start.4 = (bf16[640,512]{1,0:T(8,128)(2,1)}, bf16[640,512]{1,0:T(8,128)(2,1)S(1)}, u32[]{:S(2)}) copy-start(bf16[640,512]{1,0:T(8,128)(2,1)S(1)} %get-tuple-element.11) | copy-start | bytes 1966084
  93.4 93.0 %collective-permute-start.17 = (bf16[640,512]{1,0:T(8,128)(2,1)S(1)}, bf16[640,512]{1,0:T(8,128)(2,1)S(1)}, u32[]{:S(2)}, u32[]{:S(2)}) collective-permute-start(bf16[640,512]{1,0:T(8,128)(2,1)S(1)} %get-tuple-element.11), channel_id=1, source_target_pairs={{0,4},{4,0},{8,12},{12,8},{16,20},{20,16},{24,28},{28,24},{1,5},{5... | collective-permute-start | bytes 1966088 | tf_op jit(solution)/shard_map/ppermute | solution.py:56
  93.9 92.5 %collective-permute-start.18 = (bf16[640,512]{1,0:T(8,128)(2,1)S(1)}, bf16[640,512]{1,0:T(8,128)(2,1)}, u32[]{:S(2)}, u32[]{:S(2)}) collective-permute-start(bf16[640,512]{1,0:T(8,128)(2,1)S(1)} %get-tuple-element.10), channel_id=1, source_target_pairs={{0,8},{4,12},{8,16},{12,20},{16,24},{20,28},{24,0},{28,4},{1,9},{5... | collective-permute-start | bytes 1966088 | tf_op jit(solution)/shard_map/ppermute | solution.py:53
  176.1 26.2 %collective-permute-start.20 = (bf16[640,512]{1,0:T(8,128)(2,1)S(1)}, bf16[640,512]{1,0:T(8,128)(2,1)}, u32[]{:S(2)}, u32[]{:S(2)}) collective-permute-start(bf16[640,512]{1,0:T(8,128)(2,1)S(1)} %get-tuple-element.12), channel_id=1, source_target_pairs={{0,16},{4,20},{8,24},{12,28},{16,0},{20,4},{24,8},{28,12},{1,17},{... | collective-permute-start | bytes 1966088 | tf_op jit(solution)/shard_map/ppermute | solution.py:53
  181.8 34.2 %collective-permute-start.22 = (bf16[640,512]{1,0:T(8,128)(2,1)S(1)}, bf16[640,512]{1,0:T(8,128)(2,1)}, u32[]{:S(2)}, u32[]{:S(2)}) collective-permute-start(bf16[640,512]{1,0:T(8,128)(2,1)S(1)} %get-tuple-element.9), channel_id=1, source_target_pairs={{0,24},{4,28},{8,0},{12,4},{16,8},{20,12},{24,16},{28,20},{1,25},{... | collective-permute-start | bytes 1966088 | tf_op jit(solution)/shard_map/ppermute | solution.py:53
  186.4 0.9 copy-start.7
  186.4 275.5 %collective-permute-start.6 = (bf16[2048,1024]{1,0:T(8,128)(2,1)}, bf16[2048,1024]{1,0:T(8,128)(2,1)}, u32[]{:S(2)}, u32[]{:S(2)}) collective-permute-start(bf16[2048,1024]{1,0:T(8,128)(2,1)} %pad_maximum_fusion.1), channel_id=1, source_target_pairs={{0,1},{1,0},{2,3},{3,2},{4,5},{5,4},{6,7},{7,6},{8,9},{9,8},{10,11... | collective-permute-start | bytes 12582920 | tf_op jit(solution)/shard_map/ppermute | solution.py:66
  186.4 275.5 %collective-permute-start.9 = (bf16[2048,1024]{1,0:T(8,128)(2,1)}, bf16[2048,1024]{1,0:T(8,128)(2,1)}, u32[]{:S(2)}, u32[]{:S(2)}) collective-permute-start(bf16[2048,1024]{1,0:T(8,128)(2,1)} %constant_dynamic-update-slice_fusion), channel_id=1, source_target_pairs={{0,1},{1,0},{2,3},{3,2},{4,5},{5,4},{6,7},{7,6},{8,9},{9,8},{10,11... | collective-permute-start | bytes 12582920 | tf_op jit(solution)/shard_map/ppermute | solution.py:66
  202.3 46.4 %collective-permute-start.11 = (bf16[1024,640]{1,0:T(8,128)(2,1)S(1)}, bf16[1024,640]{1,0:T(8,128)(2,1)}, u32[]{:S(2)}, u32[]{:S(2)}) collective-permute-start(bf16[1024,640]{1,0:T(8,128)(2,1)S(1)} %pad_maximum_fusion.4), channel_id=1, source_target_pairs={{0,8},{4,12},{8,16},{12,20},{16,24},{20,28},{24,0},{28,4},{1,9},{5... | collective-permute-start | bytes 3932168 | tf_op jit(solution)/shard_map/ppermute | solution.py:53
  216.1 87.7 %collective-permute-start.13 = (bf16[1024,640]{1,0:T(8,128)(2,1)S(1)}, bf16[1024,640]{1,0:T(8,128)(2,1)}, u32[]{:S(2)}, u32[]{:S(2)}) collective-permute-start(bf16[1024,640]{1,0:T(8,128)(2,1)S(1)} %pad_maximum_fusion.5), channel_id=1, source_target_pairs={{0,16},{4,20},{8,24},{12,28},{16,0},{20,4},{24,8},{28,12},{1,17},{... | collective-permute-start | bytes 3932168 | tf_op jit(solution)/shard_map/ppermute | solution.py:53
  219.8 85.6 %collective-permute-start.15 = (bf16[1024,640]{1,0:T(8,128)(2,1)S(1)}, bf16[1024,640]{1,0:T(8,128)(2,1)}, u32[]{:S(2)}, u32[]{:S(2)}) collective-permute-start(bf16[1024,640]{1,0:T(8,128)(2,1)S(1)} %pad_maximum_fusion.6), channel_id=1, source_target_pairs={{0,24},{4,28},{8,0},{12,4},{16,8},{20,12},{24,16},{28,20},{1,25},{... | collective-permute-start | bytes 3932168 | tf_op jit(solution)/shard_map/ppermute | solution.py:53
  248.7 86.0 %collective-permute-start.19 = (bf16[640,512]{1,0:T(8,128)(2,1)}, bf16[640,512]{1,0:T(8,128)(2,1)}, u32[]{:S(2)}, u32[]{:S(2)}) collective-permute-start(bf16[640,512]{1,0:T(8,128)(2,1)} %collective-permute-done.18), channel_id=1, source_target_pairs={{0,4},{4,0},{8,12},{12,8},{16,20},{20,16},{24,28},{28,24},{1,5},{5... | collective-permute-start | bytes 1966088 | tf_op jit(solution)/shard_map/ppermute | solution.py:56
  303.8 46.5 %collective-permute-start.21 = (bf16[640,512]{1,0:T(8,128)(2,1)}, bf16[640,512]{1,0:T(8,128)(2,1)}, u32[]{:S(2)}, u32[]{:S(2)}) collective-permute-start(bf16[640,512]{1,0:T(8,128)(2,1)} %collective-permute-done.20), channel_id=1, source_target_pairs={{0,4},{4,0},{8,12},{12,8},{16,20},{20,16},{24,28},{28,24},{1,5},{5... | collective-permute-start | bytes 1966088 | tf_op jit(solution)/shard_map/ppermute | solution.py:56
  305.3 56.3 %collective-permute-start.23 = (bf16[640,512]{1,0:T(8,128)(2,1)}, bf16[640,512]{1,0:T(8,128)(2,1)}, u32[]{:S(2)}, u32[]{:S(2)}) collective-permute-start(bf16[640,512]{1,0:T(8,128)(2,1)} %collective-permute-done.22), channel_id=1, source_target_pairs={{0,4},{4,0},{8,12},{12,8},{16,20},{20,16},{24,28},{28,24},{1,5},{5... | collective-permute-start | bytes 1966088 | tf_op jit(solution)/shard_map/ppermute | solution.py:56
  315.6 14.0 %copy-start.8 = (bf16[1024]{0:T(1024)(128)(2,1)S(1)}, bf16[1024]{0:T(1024)(128)(2,1)}, u32[]{:S(2)}) copy-start(bf16[1024]{0:T(1024)(128)(2,1)} %param.6) | copy-start | bytes 6148
  334.7 78.1 %collective-permute-start.12 = (bf16[1024,640]{1,0:T(8,128)(2,1)}, bf16[1024,640]{1,0:T(8,128)(2,1)}, u32[]{:S(2)}, u32[]{:S(2)}) collective-permute-start(bf16[1024,640]{1,0:T(8,128)(2,1)} %collective-permute-done.11), channel_id=1, source_target_pairs={{0,4},{4,0},{8,12},{12,8},{16,20},{20,16},{24,28},{28,24},{1,5},{5... | collective-permute-start | bytes 3932168 | tf_op jit(solution)/shard_map/ppermute | solution.py:56
  350.3 81.7 %collective-permute-start.14 = (bf16[1024,640]{1,0:T(8,128)(2,1)}, bf16[1024,640]{1,0:T(8,128)(2,1)}, u32[]{:S(2)}, u32[]{:S(2)}) collective-permute-start(bf16[1024,640]{1,0:T(8,128)(2,1)} %collective-permute-done.13), channel_id=1, source_target_pairs={{0,4},{4,0},{8,12},{12,8},{16,20},{20,16},{24,28},{28,24},{1,5},{5... | collective-permute-start | bytes 3932168 | tf_op jit(solution)/shard_map/ppermute | solution.py:56
  361.6 89.5 %collective-permute-start.16 = (bf16[1024,640]{1,0:T(8,128)(2,1)}, bf16[1024,640]{1,0:T(8,128)(2,1)}, u32[]{:S(2)}, u32[]{:S(2)}) collective-permute-start(bf16[1024,640]{1,0:T(8,128)(2,1)} %collective-permute-done.15), channel_id=1, source_target_pairs={{0,4},{4,0},{8,12},{12,8},{16,20},{20,16},{24,28},{28,24},{1,5},{5... | collective-permute-start | bytes 3932168 | tf_op jit(solution)/shard_map/ppermute | solution.py:56
  490.1 19.6 %copy-start = (bf16[2048,4096]{1,0:T(8,128)(2,1)S(1)}, bf16[2048,4096]{1,0:T(8,128)(2,1)}, u32[]{:S(2)}) copy-start(bf16[2048,4096]{1,0:T(8,128)(2,1)} %get-tuple-element.6) | copy-start | bytes 50331652
  490.2 37.3 %slice-start = ((s8[5242880]{0:T(1024)(128)(4,1)}), s8[4194304]{0:T(1024)(128)(4,1)S(1)}, s32[]{:S(2)}) async-start(s8[5242880]{0:T(1024)(128)(4,1)} %bitcast.11), calls=%async_computation | async-start | bytes 8388608
  509.7 17.7 %slice-start.1 = ((s8[5242880]{0:T(1024)(128)(4,1)}), s8[1048576]{0:T(1024)(128)(4,1)S(1)}, s32[]{:S(2)}) async-start(s8[5242880]{0:T(1024)(128)(4,1)} %bitcast.11), calls=%async_computation.1 | async-start | bytes 2097152
  531.1 7.2 %collective-permute-start.32 = (bf16[1024,2048]{1,0:T(8,128)(2,1)S(1)}, bf16[1024,2048]{1,0:T(8,128)(2,1)S(1)}, u32[]{:S(2)}, u32[]{:S(2)}) collective-permute-start(bf16[1024,2048]{1,0:T(8,128)(2,1)S(1)} %convolution_convert_fusion), channel_id=1, source_target_pairs={{0,1},{1,0},{2,3},{3,2},{4,5},{5,4},{6,7},{7,6},{8,9},{9,8},{10,11... | collective-permute-start | bytes 12582920 | tf_op jit(solution)/shard_map/ppermute | solution.py:66
  534.9 9.5 %collective-permute-start.24 = (bf16[1024,2048]{1,0:T(8,128)(2,1)S(1)}, bf16[1024,2048]{1,0:T(8,128)(2,1)S(1)}, u32[]{:S(2)}, u32[]{:S(2)}) collective-permute-start(bf16[1024,2048]{1,0:T(8,128)(2,1)S(1)} %convolution_convert_fusion.1), channel_id=1, source_target_pairs={{0,1},{1,0},{2,3},{3,2},{4,5},{5,4},{6,7},{7,6},{8,9},{9,8},{10,11... | collective-permute-start | bytes 12582920 | tf_op jit(solution)/shard_map/ppermute | solution.py:66
  540.2 48.6 %collective-permute-start.33 = (bf16[1024,1024]{1,0:T(8,128)(2,1)S(1)}, bf16[1024,1024]{1,0:T(8,128)(2,1)S(1)}, u32[]{:S(2)}, u32[]{:S(2)}) collective-permute-start(bf16[1024,1024]{1,0:T(8,128)(2,1)S(1)} %add_convert_fusion.1), channel_id=1, source_target_pairs={{0,2},{1,3},{2,0},{3,1},{4,6},{5,7},{6,4},{7,5},{8,10},{9,11},{10,... | collective-permute-start | bytes 6291464 | tf_op jit(solution)/shard_map/ppermute | solution.py:61
  546.2 86.7 %collective-permute-start.25 = (bf16[1024,1024]{1,0:T(8,128)(2,1)S(1)}, bf16[1024,1024]{1,0:T(8,128)(2,1)S(1)}, u32[]{:S(2)}, u32[]{:S(2)}) collective-permute-start(bf16[1024,1024]{1,0:T(8,128)(2,1)S(1)} %add_convert_fusion.3), channel_id=1, source_target_pairs={{0,2},{1,3},{2,0},{3,1},{4,6},{5,7},{6,4},{7,5},{8,10},{9,11},{10,... | collective-permute-start | bytes 6291464 | tf_op jit(solution)/shard_map/ppermute | solution.py:61
  590.8 73.8 %collective-permute-start.34 = (bf16[256,1024]{1,0:T(8,128)(2,1)S(1)}, bf16[256,1024]{1,0:T(8,128)(2,1)S(1)}, u32[]{:S(2)}, u32[]{:S(2)}) collective-permute-start(bf16[256,1024]{1,0:T(8,128)(2,1)S(1)} %get-tuple-element.31), channel_id=1, source_target_pairs={{0,8},{4,12},{1,9},{5,13},{2,10},{6,14},{3,11},{7,15}} | collective-permute-start | bytes 1572872 | tf_op jit(solution)/shard_map/ppermute | solution.py:49
  619.8 44.8 %collective-permute-start.37 = (bf16[256,1024]{1,0:T(8,128)(2,1)S(1)}, bf16[256,1024]{1,0:T(8,128)(2,1)S(1)}, u32[]{:S(2)}, u32[]{:S(2)}) collective-permute-start(bf16[256,1024]{1,0:T(8,128)(2,1)S(1)} %get-tuple-element.32), channel_id=1, source_target_pairs={{24,16},{28,20},{25,17},{29,21},{26,18},{30,22},{27,19},{31,23}} | collective-permute-start | bytes 1572872 | tf_op jit(solution)/shard_map/ppermute | solution.py:49
  634.9 41.3 %collective-permute-start.26 = (bf16[256,1024]{1,0:T(8,128)(2,1)S(1)}, bf16[256,1024]{1,0:T(8,128)(2,1)S(1)}, u32[]{:S(2)}, u32[]{:S(2)}) collective-permute-start(bf16[256,1024]{1,0:T(8,128)(2,1)S(1)} %get-tuple-element.25), channel_id=1, source_target_pairs={{0,8},{4,12},{1,9},{5,13},{2,10},{6,14},{3,11},{7,15}} | collective-permute-start | bytes 1572872 | tf_op jit(solution)/shard_map/ppermute | solution.py:49
  663.9 12.3 %collective-permute-start.29 = (bf16[256,1024]{1,0:T(8,128)(2,1)S(1)}, bf16[256,1024]{1,0:T(8,128)(2,1)S(1)}, u32[]{:S(2)}, u32[]{:S(2)}) collective-permute-start(bf16[256,1024]{1,0:T(8,128)(2,1)S(1)} %get-tuple-element.26), channel_id=1, source_target_pairs={{24,16},{28,20},{25,17},{29,21},{26,18},{30,22},{27,19},{31,23}} | collective-permute-start | bytes 1572872 | tf_op jit(solution)/shard_map/ppermute | solution.py:49
  665.0 22.4 %collective-permute-start.35 = (bf16[256,1024]{1,0:T(8,128)(2,1)S(1)}, bf16[256,1024]{1,0:T(8,128)(2,1)S(1)}, u32[]{:S(2)}, u32[]{:S(2)}) collective-permute-start(bf16[256,1024]{1,0:T(8,128)(2,1)S(1)} %get-tuple-element.29), channel_id=1, source_target_pairs={{0,8},{4,12},{8,16},{12,20},{1,9},{5,13},{9,17},{13,21},{2,10},{6,... | collective-permute-start | bytes 1572872 | tf_op jit(solution)/shard_map/ppermute | solution.py:49
  666.3 21.1 %collective-permute-start.38 = (bf16[256,1024]{1,0:T(8,128)(2,1)S(1)}, bf16[256,1024]{1,0:T(8,128)(2,1)S(1)}, u32[]{:S(2)}, u32[]{:S(2)}) collective-permute-start(bf16[256,1024]{1,0:T(8,128)(2,1)S(1)} %get-tuple-element.30), channel_id=1, source_target_pairs={{16,8},{20,12},{24,16},{28,20},{17,9},{21,13},{25,17},{29,21},{18,... | collective-permute-start | bytes 1572872 | tf_op jit(solution)/shard_map/ppermute | solution.py:49
  676.5 22.2 %collective-permute-start.27 = (bf16[256,1024]{1,0:T(8,128)(2,1)S(1)}, bf16[256,1024]{1,0:T(8,128)(2,1)S(1)}, u32[]{:S(2)}, u32[]{:S(2)}) collective-permute-start(bf16[256,1024]{1,0:T(8,128)(2,1)S(1)} %get-tuple-element.23), channel_id=1, source_target_pairs={{0,8},{4,12},{8,16},{12,20},{1,9},{5,13},{9,17},{13,21},{2,10},{6,... | collective-permute-start | bytes 1572872 | tf_op jit(solution)/shard_map/ppermute | solution.py:49
  680.9 17.8 %collective-permute-start.30 = (bf16[256,1024]{1,0:T(8,128)(2,1)S(1)}, bf16[256,1024]{1,0:T(8,128)(2,1)S(1)}, u32[]{:S(2)}, u32[]{:S(2)}) collective-permute-start(bf16[256,1024]{1,0:T(8,128)(2,1)S(1)} %get-tuple-element.24), channel_id=1, source_target_pairs={{16,8},{20,12},{24,16},{28,20},{17,9},{21,13},{25,17},{29,21},{18,... | collective-permute-start | bytes 1572872 | tf_op jit(solution)/shard_map/ppermute | solution.py:49
  687.8 17.6 %collective-permute-start.39 = (bf16[256,1024]{1,0:T(8,128)(2,1)S(1)}, bf16[256,1024]{1,0:T(8,128)(2,1)S(1)}, u32[]{:S(2)}, u32[]{:S(2)}) collective-permute-start(bf16[256,1024]{1,0:T(8,128)(2,1)S(1)} %get-tuple-element.28), channel_id=1, source_target_pairs={{8,0},{12,4},{16,8},{20,12},{24,16},{28,20},{9,1},{13,5},{17,9},{2... | collective-permute-start | bytes 1572872 | tf_op jit(solution)/shard_map/ppermute | solution.py:49
  689.1 20.8 %collective-permute-start.36 = (bf16[256,1024]{1,0:T(8,128)(2,1)S(1)}, bf16[256,1024]{1,0:T(8,128)(2,1)S(1)}, u32[]{:S(2)}, u32[]{:S(2)}) collective-permute-start(bf16[256,1024]{1,0:T(8,128)(2,1)S(1)} %get-tuple-element.27), channel_id=1, source_target_pairs={{0,8},{4,12},{8,16},{12,20},{16,24},{20,28},{1,9},{5,13},{9,17},{1... | collective-permute-start | bytes 1572872 | tf_op jit(solution)/shard_map/ppermute | solution.py:49
  699.0 13.2 %collective-permute-start.31 = (bf16[256,1024]{1,0:T(8,128)(2,1)S(1)}, bf16[256,1024]{1,0:T(8,128)(2,1)S(1)}, u32[]{:S(2)}, u32[]{:S(2)}) collective-permute-start(bf16[256,1024]{1,0:T(8,128)(2,1)S(1)} %get-tuple-element.22), channel_id=1, source_target_pairs={{8,0},{12,4},{16,8},{20,12},{24,16},{28,20},{9,1},{13,5},{17,9},{2... | collective-permute-start | bytes 1572872 | tf_op jit(solution)/shard_map/ppermute | solution.py:49
  700.3 19.1 %collective-permute-start.28 = (bf16[256,1024]{1,0:T(8,128)(2,1)S(1)}, bf16[256,1024]{1,0:T(8,128)(2,1)S(1)}, u32[]{:S(2)}, u32[]{:S(2)}) collective-permute-start(bf16[256,1024]{1,0:T(8,128)(2,1)S(1)} %get-tuple-element.21), channel_id=1, source_target_pairs={{0,8},{4,12},{8,16},{12,20},{16,24},{20,28},{1,9},{5,13},{9,17},{1... | collective-permute-start | bytes 1572872 | tf_op jit(solution)/shard_map/ppermute | solution.py:49
where the time goes:
time: 724 us; the launch traced here: 721 us
  waiting for transfers between devices  343 us (47%)
  local copies, waits for them, and re-layouts  158 us (22%)
  starting transfers between devices  123 us (17%)
  matrix products  51.9 us (7%)
  other arithmetic  39.9 us (6%)
    ppermute x4, waiting for transfers between devices, other_x(): lax.ppermute(value, 'col', [(a * cores + b, (1 - a) * cores + b) for a in...  136 us
    ppermute x18, waiting for transfers between devices, along_z(): return lax.ppermute(value, 'row', pairs)  103 us
    ppermute x6, waiting for transfers between devices, round_z(): return lax.ppermute(value, 'row', pairs)  97.4 us
    ppermute x18, starting transfers between devices, along_z(): return lax.ppermute(value, 'row', pairs)  90.7 us
    dynamic_update_slice x8, local copies, waits for them, and re-layouts, spread(): output_all = lax.dynamic_update_slice_in_dim(output_all, piece, place, 1)  54.9 us
    dot_general x8, matrix products, dot(): return jnp.dot(left, right, preferred_element_type=jnp.float32)  51.9 us
    dynamic_update_slice x8, local copies, waits for them, and re-layouts, spread(): lax.dynamic_update_slice_in_dim(linear_all, piece[depth:], place, 0)  33.3 us
    dynamic_update_slice x8, local copies, waits for them, and re-layouts, spread(): lax.dynamic_update_slice_in_dim(gate_all, piece[:depth], place, 0)  33.2 us
  transfers between devices with their start and end apart: 40, of which 18 were waited for; matrix products, arithmetic and copies ran while one was open for 24% of the time, Pallas kernels for 0%

commit v1 on v0

--- a/solution.py
+++ b/solution.py
@@ -110,18 +110,22 @@
         ],
     )
     outputs = both_y([piece_of(output_weight, 0, step) for step in range(zs)])
-    part = gate_weight.shape[1] // zs
 
-    gate_all = jnp.zeros((width * xs * cores, part), gate_weight.dtype)
-    linear_all, output_all = gate_all, jnp.zeros((part, width * xs * cores), gate_weight.dtype)
-    for origin, piece in inputs:
-        place = ((origin * depth // width) ^ col) * width + origin * depth % width
-        gate_all = lax.dynamic_update_slice_in_dim(gate_all, piece[:depth], place, 0)
-        linear_all = lax.dynamic_update_slice_in_dim(linear_all, piece[depth:], place, 0)
-    for origin, piece in outputs:
-        k = (origin * depth // width) ^ col
-        place = ((1 - k % cores) * xs + k // cores) * width + origin * depth % width
-        output_all = lax.dynamic_update_slice_in_dim(output_all, piece, place, 1)
+    def joined(found, dim, order, cut=slice(None)):
+        steps = []
+        for step in range(zs):
+            own, passed = found[2 * step][1][cut], found[2 * step + 1][1][cut]
+            steps += [jnp.where(y == 0, own, passed), jnp.where(y == 0, passed, own)]
+        stack = jnp.concatenate(steps, axis=dim)
+        blocks = [
+            lax.dynamic_slice_in_dim(stack, (z - (col ^ k)) % zs * width, width, dim) for k in order
+        ]
+        return jnp.concatenate(blocks, axis=dim)
+
+    near = range(xs * cores)
+    gate_all = joined(inputs, 0, near, slice(0, depth))
+    linear_all = joined(inputs, 0, near, slice(depth, None))
+    output_all = joined(outputs, 1, [k for c in range(cores - 1, -1, -1) for k in near[c::cores]])
 
     normed = rms_normed(whole, gain_all)
     gate = dot(normed, gate_all)
@@ -164,7 +168,7 @@
     zs, ys, xs, cores = rows // 2, 2, cols // 2, 2
 
     def fits(gate_weight):
-        return xs == 2 and gate_weight[1] // cols % (zs * LANES) == 0
+        return xs == 2 and zs == cols and gate_weight[1] // cols % (zs * LANES) == 0
 
     def local(tokens, norm_gain, gate_weight, linear_weight, output_weight):
         args = (tokens, norm_gain, gate_weight, linear_weight, output_weight)

time: 724 us -> 552 us (0.76)
  local copies, waits for them, and re-layouts: 158 us -> 15.7 us
  starting transfers between devices: 123 us -> 65.2 us
  other arithmetic: 39.9 us -> 56.2 us
  blocking collectives: 5.18 us -> 15.1 us
  waiting for transfers between devices: 343 us -> 334 us
  matrix products: 51.9 us -> 59.9 us
    dynamic_update_slice x24 -> x0, local copies, waits for them, and re-layouts: 121 us -> none  [the longest x8 54.9 us: spread(): output_all = lax.dynamic_update_slice_in_dim(output_all, piece, place, 1)]
    ppermute x8, waiting for transfers between devices: 0.02 us -> 89.8 us  [other_y(): lax.ppermute(value, 'row', [(a * ys + b, a * ys + 1 - b) for a in range(z...]
    ppermute x4, waiting for transfers between devices: 136 us -> 77.3 us  [other_x(): lax.ppermute(value, 'col', [(a * cores + b, (1 - a) * cores + b) for a in...]
    ppermute x18, starting transfers between devices: 90.7 us -> 40.8 us  [along_z(): return lax.ppermute(value, 'row', pairs)]
    ppermute x6, waiting for transfers between devices: 97.4 us -> 72.3 us  [round_z(): return lax.ppermute(value, 'row', pairs)]
    slice x7 -> x0, local copies, waits for them, and re-layouts: 17.4 us -> none  [spread(): piece[depth:]]
    ppermute x18, waiting for transfers between devices: 103 us -> 91 us  [along_z(): return lax.ppermute(value, 'row', pairs)]
    ppermute x6, starting transfers between devices: 17.9 us -> 7.25 us  [round_z(): return lax.ppermute(value, 'row', pairs)]
  transfers between devices with their start and end apart: 40 -> 40, of which waited for: 18 -> 21; matrix products, arithmetic and copies ran while one was open for 24% -> 9% of each run, Pallas kernels for 0% -> 0%
where the time goes in v1:
time: 552 us; the launch traced here: 547 us
  waiting for transfers between devices  334 us (61%)
  starting transfers between devices  65.2 us (12%)
  matrix products  59.9 us (11%)
  other arithmetic  56.2 us (10%)
  local copies, waits for them, and re-layouts  15.7 us (3%)
  blocking collectives  15.1 us (3%)
    ppermute x18, waiting for transfers between devices, along_z(): return lax.ppermute(value, 'row', pairs)  91 us
    ppermute x8, waiting for transfers between devices, other_y(): lax.ppermute(value, 'row', [(a * ys + b, a * ys + 1 - b) for a in range(z...  89.8 us
    ppermute x4, waiting for transfers between devices, other_x(): lax.ppermute(value, 'col', [(a * cores + b, (1 - a) * cores + b) for a in...  77.3 us
    ppermute x6, waiting for transfers between devices, round_z(): return lax.ppermute(value, 'row', pairs)  72.3 us
    dot_general x8, matrix products, dot(): return jnp.dot(left, right, preferred_element_type=jnp.float32)  59.9 us
    ppermute x18, starting transfers between devices, along_z(): return lax.ppermute(value, 'row', pairs)  40.8 us
    reduce_sum x1, other arithmetic, rms_normed(): meansq = jnp.mean(values * values, axis=-1, keepdims=True)  35.7 us
    all_gather x1, blocking collectives, spread(): gains = lax.all_gather(norm_gain, 'col', axis=0, tiled=True)  15.1 us
  transfers between devices with their start and end apart: 40, of which 21 were waited for; matrix products, arithmetic and copies ran while one was open for 9% of the time, Pallas kernels for 0%

profile of v1, /device:TPU:0, one launch (start us, length us, event | category | flops | bytes accessed | tf_op | source)
XLA Modules:
  0.0 547.3 jit_solution(11296987953925938098)
XLA Ops:
  0.0 5.1 collective-permute-start
  5.2 1.3 collective-permute-start.1
  6.5 21.3 %collective-permute-done = bf16[512,1024]{1,0:T(8,128)(2,1)S(1)} collective-permute-done((bf16[512,1024]{1,0:T(8,128)(2,1)}, bf16[512,1024]{1,0:T(8,128)(2,1)S(1)}, u32[]{:S(2)}, u32[]{:S(2)}) %collective-permute-start) | collective-permute-done | bytes 1048608 | tf_op jit(solution)/shard_map/ppermute | solution.py:49
  28.8 1.6 collective-permute-start.4
  30.5 1.4 collective-permute-done.1
  31.9 1.3 collective-permute-start.2
  33.2 1.7 collective-permute-start.5
  34.9 24.8 %collective-permute-done.2 = bf16[512,1024]{1,0:T(8,128)(2,1)} collective-permute-done((bf16[512,1024]{1,0:T(8,128)(2,1)S(1)}, bf16[512,1024]{1,0:T(8,128)(2,1)}, u32[]{:S(2)}, u32[]{:S(2)}) %collective-permute-start.2) | collective-permute-done | bytes 1048608 | tf_op jit(solution)/shard_map/ppermute | solution.py:49
  61.0 1.6 collective-permute-start.7
  62.5 2.7 constant_dynamic-slice_fusion.2
  65.2 1.5 collective-permute-start.17
  66.8 3.6 collective-permute-start.18
  70.3 15.1 %all_gather.3 = bf16[4096]{0:T(1024)(128)(2,1)S(1)} all-gather(bf16[1024]{0:T(1024)(128)(2,1)S(1)} %copy-done.7), channel_id=1, replica_groups=mesh['row'=8,'col'=4] {'col'}, dimensions={0}, use_global_device_ids=true | all-gather | bytes 10240 | tf_op jit(solution)/shard_map/all_gather | solution.py:87
  85.4 1.3 broadcast_select_fusion.1
  86.8 3.1 collective-permute-start.20
  89.9 1.3 broadcast_select_fusion
  91.3 10.2 %collective-permute-done.3 = bf16[512,1024]{1,0:T(8,128)(2,1)} collective-permute-done((bf16[512,1024]{1,0:T(8,128)(2,1)}, bf16[512,1024]{1,0:T(8,128)(2,1)}, u32[]{:S(2)}, u32[]{:S(2)}) %collective-permute-start.3) | collective-permute-done | bytes 1048608 | tf_op jit(solution)/shard_map/ppermute | solution.py:49
  101.5 1.3 broadcast_select_fusion.2
  103.2 1.6 collective-permute-start.8
  105.8 1.6 collective-permute-start.19
  109.7 37.6 %collective-permute-done.20 = bf16[640,512]{1,0:T(8,128)(2,1)S(1)} collective-permute-done((bf16[640,512]{1,0:T(8,128)(2,1)S(1)}, bf16[640,512]{1,0:T(8,128)(2,1)S(1)}, u32[]{:S(2)}, u32[]{:S(2)}) %collective-permute-start.20) | collective-permute-done | bytes 655392 | tf_op jit(solution)/shard_map/ppermute | solution.py:53
  147.3 1.5 collective-permute-start.10
  149.3 1.3 constant_dynamic-update-slice_fusion.1
  152.8 39.0 %collective-permute-done.21 = bf16[640,512]{1,0:T(8,128)(2,1)S(1)} collective-permute-done((bf16[640,512]{1,0:T(8,128)(2,1)S(1)}, bf16[640,512]{1,0:T(8,128)(2,1)S(1)}, u32[]{:S(2)}, u32[]{:S(2)}) %collective-permute-start.21) | collective-permute-done | bytes 655392 | tf_op jit(solution)/shard_map/ppermute | solution.py:56
  194.4 1.5 collective-permute-start.23
  197.4 14.6 %collective-permute-done.23 = bf16[640,512]{1,0:T(8,128)(2,1)S(1)} collective-permute-done((bf16[640,512]{1,0:T(8,128)(2,1)S(1)}, bf16[640,512]{1,0:T(8,128)(2,1)S(1)}, u32[]{:S(2)}, u32[]{:S(2)}) %collective-permute-start.23) | collective-permute-done | bytes 655392 | tf_op jit(solution)/shard_map/ppermute | solution.py:56
  214.2 10.2 %collective-permute-done.13 = bf16[1024,640]{1,0:T(8,128)(2,1)S(1)} collective-permute-done((bf16[1024,640]{1,0:T(8,128)(2,1)S(1)}, bf16[1024,640]{1,0:T(8,128)(2,1)S(1)}, u32[]{:S(2)}, u32[]{:S(2)}) %collective-permute-start.13) | collective-permute-done | bytes 1310752 | tf_op jit(solution)/shard_map/ppermute | solution.py:53
  224.4 1.5 collective-permute-start.14
  225.9 24.5 %collective-permute-done.15 = bf16[1024,640]{1,0:T(8,128)(2,1)S(1)} collective-permute-done((bf16[1024,640]{1,0:T(8,128)(2,1)S(1)}, bf16[1024,640]{1,0:T(8,128)(2,1)S(1)}, u32[]{:S(2)}, u32[]{:S(2)}) %collective-permute-start.15) | collective-permute-done | bytes 1310752 | tf_op jit(solution)/shard_map/ppermute | solution.py:53
  250.4 1.5 collective-permute-start.16
  252.2 3.5 constant_dynamic-slice_fusion.1
  257.0 11.2 %collective-permute-done.14 = bf16[1024,640]{1,0:T(8,128)(2,1)S(1)} collective-permute-done((bf16[1024,640]{1,0:T(8,128)(2,1)S(1)}, bf16[1024,640]{1,0:T(8,128)(2,1)S(1)}, u32[]{:S(2)}, u32[]{:S(2)}) %collective-permute-start.14) | collective-permute-done | bytes 1310752 | tf_op jit(solution)/shard_map/ppermute | solution.py:56
  269.1 25.1 %collective-permute-done.16 = bf16[1024,640]{1,0:T(8,128)(2,1)S(1)} collective-permute-done((bf16[1024,640]{1,0:T(8,128)(2,1)S(1)}, bf16[1024,640]{1,0:T(8,128)(2,1)S(1)}, u32[]{:S(2)}, u32[]{:S(2)}) %collective-permute-start.16) | collective-permute-done | bytes 1310752 | tf_op jit(solution)/shard_map/ppermute | solution.py:56
  295.1 2.1 constant_dynamic-slice_fusion.13
  297.2 2.4 constant_dynamic-slice_fusion.9
  299.6 35.7 %fusion = (f32[2048]{0:T(1024)S(1)}, bf16[2048,4096]{1,0:T(8,128)(2,1)}) fusion(bf16[2048,1024]{1,0:T(8,128)(2,1)} %collective-permute-done.9, bf16[2048,1024]{1,0:T(8,128)(2,1)S(1)} %constant_dynamic-update-slice_fusion, bf16[2048,1024]{1,0:T(8,128)(2,1)} %collective-permute-done.6, bf16[512,1024]{1,0:T(8,128)(2,1)S(1)} %broadcast_select_fusion, ...), kind=kLoop, calls=%fused_computation.2 | loop fusion | flops 142604288 | bytes 33562624 | tf_op jit(solution)/shard_map/reduce_sum | solution.py:28
  335.3 19.8 %fusion.12 = f32[2048,640]{1,0:T(8,128)} fusion(bf16[1024,640]{1,0:T(8,128)(2,1)} %get-tuple-element.14, bf16[1024,640]{1,0:T(8,128)(2,1)} %get-tuple-element.15, bf16[1024,640]{1,0:T(8,128)(2,1)} %get-tuple-element.16, bf16[1024,640]{1,0:T(8,128)(2,1)S(1)} %get-tuple-element.13, bf16[2048,4096]{1,0:T(8,128)(2,1)} %get-tuple-element.6, ...), kind=kOutput, calls=%fused_computation.16 | convolution fusion | flops 10791944192 | bytes 27287552 | tf_op jit(solution)/shard_map/dot_general | solution.py:23
  355.1 19.6 %fusion.11 = bf16[2048,640]{1,0:T(8,128)(2,1)S(1)} fusion(f32[2048,640]{1,0:T(8,128)} %fusion.12, bf16[1024,640]{1,0:T(8,128)(2,1)} %get-tuple-element.10, bf16[1024,640]{1,0:T(8,128)(2,1)} %get-tuple-element.11, bf16[1024,640]{1,0:T(8,128)(2,1)} %get-tuple-element.12, bf16[1024,640]{1,0:T(8,128)(2,1)} %get-tuple-element.9, ...), kind=kOutput, calls=%fused_computation.15 | convolution fusion | flops 10805051392 | bytes 29908992 | tf_op jit(solution)/shard_map/dot_general | solution.py:23
  376.4 3.8 convolution_convert_fusion
  380.2 4.0 convolution_convert_fusion.1
  384.8 2.6 collective-permute-done.32
  387.4 3.1 add_convert_fusion.1
  390.5 1.6 collective-permute-start.33
  392.1 1.3 collective-permute-done.24
  393.4 3.1 add_convert_fusion.3
  396.5 1.6 collective-permute-start.25
  398.1 41.0 %collective-permute-done.33 = bf16[1024,1024]{1,0:T(8,128)(2,1)S(1)} collective-permute-done((bf16[1024,1024]{1,0:T(8,128)(2,1)S(1)}, bf16[1024,1024]{1,0:T(8,128)(2,1)S(1)}, u32[]{:S(2)}, u32[]{:S(2)}) %collective-permute-start.33) | collective-permute-done | bytes 2097184 | tf_op jit(solution)/shard_map/ppermute | solution.py:61
  439.1 3.3 add_convert_fusion
  442.5 3.7 collective-permute-start.34
  446.8 36.3 %collective-permute-done.25 = bf16[1024,1024]{1,0:T(8,128)(2,1)S(1)} collective-permute-done((bf16[1024,1024]{1,0:T(8,128)(2,1)S(1)}, bf16[1024,1024]{1,0:T(8,128)(2,1)S(1)}, u32[]{:S(2)}, u32[]{:S(2)}) %collective-permute-start.25) | collective-permute-done | bytes 2097184 | tf_op jit(solution)/shard_map/ppermute | solution.py:61
  483.2 3.3 add_convert_fusion.2
  486.6 3.7 collective-permute-start.26
  491.3 1.3 collective-permute-start.35
  493.3 9.2 %collective-permute-done.26 = bf16[256,1024]{1,0:T(8,128)(2,1)S(1)} collective-permute-done((bf16[256,1024]{1,0:T(8,128)(2,1)S(1)}, bf16[256,1024]{1,0:T(8,128)(2,1)S(1)}, u32[]{:S(2)}, u32[]{:S(2)}) %collective-permute-start.26) | collective-permute-done | bytes 524320 | tf_op jit(solution)/shard_map/ppermute | solution.py:49
  502.8 4.4 collective-permute-start.27
  508.0 5.8 %collective-permute-done.35 = bf16[256,1024]{1,0:T(8,128)(2,1)S(1)} collective-permute-done((bf16[256,1024]{1,0:T(8,128)(2,1)S(1)}, bf16[256,1024]{1,0:T(8,128)(2,1)S(1)}, u32[]{:S(2)}, u32[]{:S(2)}) %collective-permute-start.35) | collective-permute-done | bytes 524320 | tf_op jit(solution)/shard_map/ppermute | solution.py:49
  514.2 1.3 collective-permute-start.39
  515.5 5.0 collective-permute-start.36
  520.5 4.5 collective-permute-done.27
  525.4 1.3 collective-permute-start.31
  526.7 5.0 collective-permute-start.28
  531.8 4.5 collective-permute-done.36
  536.5 2.1 collective-permute-done.31
  538.6 7.2 %collective-permute-done.28 = bf16[256,1024]{1,0:T(8,128)(2,1)S(1)} collective-permute-done((bf16[256,1024]{1,0:T(8,128)(2,1)S(1)}, bf16[256,1024]{1,0:T(8,128)(2,1)S(1)}, u32[]{:S(2)}, u32[]{:S(2)}) %collective-permute-start.28) | collective-permute-done | bytes 524320 | tf_op jit(solution)/shard_map/ppermute | solution.py:49
  (90 shorter events, 26.5 us)
Async XLA Ops:
  0.0 70.3 %copy-start.7 = (bf16[1024]{0:T(1024)(128)(2,1)S(1)}, bf16[1024]{0:T(1024)(128)(2,1)}, u32[]{:S(2)}) copy-start(bf16[1024]{0:T(1024)(128)(2,1)} %param.6) | copy-start | bytes 6148
  0.0 27.8 %collective-permute-start = (bf16[512,1024]{1,0:T(8,128)(2,1)}, bf16[512,1024]{1,0:T(8,128)(2,1)S(1)}, u32[]{:S(2)}, u32[]{:S(2)}) collective-permute-start(bf16[512,1024]{1,0:T(8,128)(2,1)} %param.5), channel_id=1, source_target_pairs={{0,8},{4,12},{8,16},{12,20},{16,24},{20,28},{1,9},{5,13},{9,17},{1... | collective-permute-start | bytes 3145736 | tf_op jit(solution)/shard_map/ppermute | solution.py:49
  5.2 26.7 %collective-permute-start.1 = (bf16[512,1024]{1,0:T(8,128)(2,1)}, bf16[512,1024]{1,0:T(8,128)(2,1)S(1)}, u32[]{:S(2)}, u32[]{:S(2)}) collective-permute-start(bf16[512,1024]{1,0:T(8,128)(2,1)} %param.5), channel_id=1, source_target_pairs={{8,0},{12,4},{16,8},{20,12},{24,16},{28,20},{9,1},{13,5},{17,9},{2... | collective-permute-start | bytes 3145736 | tf_op jit(solution)/shard_map/ppermute | solution.py:49
  27.8 1.0 copy-start.5
  28.8 4.3 collective-permute-start.4
  31.9 1.3 copy-start.6
  31.9 27.8 %collective-permute-start.2 = (bf16[512,1024]{1,0:T(8,128)(2,1)S(1)}, bf16[512,1024]{1,0:T(8,128)(2,1)}, u32[]{:S(2)}, u32[]{:S(2)}) collective-permute-start(bf16[512,1024]{1,0:T(8,128)(2,1)S(1)} %collective-permute-done.1), channel_id=1, source_target_pairs={{8,0},{12,4},{16,8},{20,12},{9,1},{13,5},{17,9},{21,13},{10,2},{14... | collective-permute-start | bytes 3145736 | tf_op jit(solution)/shard_map/ppermute | solution.py:49
  33.2 53.6 %collective-permute-start.5 = (bf16[512,1024]{1,0:T(8,128)(2,1)}, bf16[512,1024]{1,0:T(8,128)(2,1)}, u32[]{:S(2)}, u32[]{:S(2)}) collective-permute-start(bf16[512,1024]{1,0:T(8,128)(2,1)} %collective-permute-done.4), channel_id=1, source_target_pairs={{16,24},{20,28},{17,25},{21,29},{18,26},{22,30},{19,27},{23,31}} | collective-permute-start | bytes 3145736 | tf_op jit(solution)/shard_map/ppermute | solution.py:49
  59.7 41.8 %collective-permute-start.3 = (bf16[512,1024]{1,0:T(8,128)(2,1)}, bf16[512,1024]{1,0:T(8,128)(2,1)}, u32[]{:S(2)}, u32[]{:S(2)}) collective-permute-start(bf16[512,1024]{1,0:T(8,128)(2,1)} %collective-permute-done.2), channel_id=1, source_target_pairs={{8,0},{12,4},{9,1},{13,5},{10,2},{14,6},{11,3},{15,7}} | collective-permute-start | bytes 3145736 | tf_op jit(solution)/shard_map/ppermute | solution.py:49
  61.0 87.9 %collective-permute-start.7 = (bf16[512,1024]{1,0:T(8,128)(2,1)}, bf16[512,1024]{1,0:T(8,128)(2,1)}, u32[]{:S(2)}, u32[]{:S(2)}) collective-permute-start(bf16[512,1024]{1,0:T(8,128)(2,1)} %param.5), channel_id=1, source_target_pairs={{0,2},{1,3},{2,0},{3,1},{4,6},{5,7},{6,4},{7,5},{8,10},{9,11},{10,... | collective-permute-start | bytes 3145736 | tf_op jit(solution)/shard_map/ppermute | solution.py:61
  65.2 40.5 %collective-permute-start.17 = (bf16[640,512]{1,0:T(8,128)(2,1)S(1)}, bf16[640,512]{1,0:T(8,128)(2,1)S(1)}, u32[]{:S(2)}, u32[]{:S(2)}) collective-permute-start(bf16[640,512]{1,0:T(8,128)(2,1)S(1)} %get-tuple-element.21), channel_id=1, source_target_pairs={{0,4},{4,0},{8,12},{12,8},{16,20},{20,16},{24,28},{28,24},{1,5},{5... | collective-permute-start | bytes 1966088 | tf_op jit(solution)/shard_map/ppermute | solution.py:56
  66.8 39.1 %collective-permute-start.18 = (bf16[640,512]{1,0:T(8,128)(2,1)}, bf16[640,512]{1,0:T(8,128)(2,1)S(1)}, u32[]{:S(2)}, u32[]{:S(2)}) collective-permute-start(bf16[640,512]{1,0:T(8,128)(2,1)} %get-tuple-element.20), channel_id=1, source_target_pairs={{0,8},{4,12},{8,16},{12,20},{16,24},{20,28},{24,0},{28,4},{1,9},{5... | collective-permute-start | bytes 1966088 | tf_op jit(solution)/shard_map/ppermute | solution.py:53
  86.8 60.5 %collective-permute-start.20 = (bf16[640,512]{1,0:T(8,128)(2,1)S(1)}, bf16[640,512]{1,0:T(8,128)(2,1)S(1)}, u32[]{:S(2)}, u32[]{:S(2)}) collective-permute-start(bf16[640,512]{1,0:T(8,128)(2,1)S(1)} %get-tuple-element.22), channel_id=1, source_target_pairs={{0,16},{4,20},{8,24},{12,28},{16,0},{20,4},{24,8},{28,12},{1,17},{... | collective-permute-start | bytes 1966088 | tf_op jit(solution)/shard_map/ppermute | solution.py:53
  91.2 13.5 %copy-start.1 = (bf16[512,2560]{1,0:T(8,128)(2,1)S(1)}, bf16[512,2560]{1,0:T(8,128)(2,1)}, u32[]{:S(2)}) copy-start(bf16[512,2560]{1,0:T(8,128)(2,1)} %param.8) | copy-start | bytes 7864324
  91.2 13.5 %copy-start.2 = (bf16[512,2560]{1,0:T(8,128)(2,1)S(1)}, bf16[512,2560]{1,0:T(8,128)(2,1)}, u32[]{:S(2)}) copy-start(bf16[512,2560]{1,0:T(8,128)(2,1)} %param.7) | copy-start | bytes 7864324
  103.2 93.2 %collective-permute-start.8 = (bf16[1536,1024]{1,0:T(8,128)(2,1)S(1)}, bf16[1536,1024]{1,0:T(8,128)(2,1)S(1)}, u32[]{:S(2)}, u32[]{:S(2)}) collective-permute-start(bf16[1536,1024]{1,0:T(8,128)(2,1)S(1)} %pad_maximum_fusion.2), channel_id=1, source_target_pairs={{0,2},{1,3},{2,0},{3,1},{4,6},{5,7},{6,4},{7,5},{8,10},{9,11},{10,... | collective-permute-start | bytes 9437192 | tf_op jit(solution)/shard_map/ppermute | solution.py:61
  105.8 88.6 %collective-permute-start.11 = (bf16[1024,640]{1,0:T(8,128)(2,1)S(1)}, bf16[1024,640]{1,0:T(8,128)(2,1)S(1)}, u32[]{:S(2)}, u32[]{:S(2)}) collective-permute-start(bf16[1024,640]{1,0:T(8,128)(2,1)S(1)} %pad_maximum_fusion.7), channel_id=1, source_target_pairs={{0,8},{4,12},{8,16},{12,20},{16,24},{20,28},{24,0},{28,4},{1,9},{5... | collective-permute-start | bytes 3932168 | tf_op jit(solution)/shard_map/ppermute | solution.py:53
  105.8 44.8 %collective-permute-start.19 = (bf16[640,512]{1,0:T(8,128)(2,1)S(1)}, bf16[640,512]{1,0:T(8,128)(2,1)S(1)}, u32[]{:S(2)}, u32[]{:S(2)}) collective-permute-start(bf16[640,512]{1,0:T(8,128)(2,1)S(1)} %collective-permute-done.18), channel_id=1, source_target_pairs={{0,4},{4,0},{8,12},{12,8},{16,20},{20,16},{24,28},{28,24},{1,5},{5... | collective-permute-start | bytes 1966088 | tf_op jit(solution)/shard_map/ppermute | solution.py:56
  147.3 50.0 %collective-permute-start.10 = (bf16[1024,640]{1,0:T(8,128)(2,1)S(1)}, bf16[1024,640]{1,0:T(8,128)(2,1)S(1)}, u32[]{:S(2)}, u32[]{:S(2)}) collective-permute-start(bf16[1024,640]{1,0:T(8,128)(2,1)S(1)} %pad_maximum_fusion.6), channel_id=1, source_target_pairs={{0,4},{4,0},{8,12},{12,8},{16,20},{20,16},{24,28},{28,24},{1,5},{5... | collective-permute-start | bytes 3932168 | tf_op jit(solution)/shard_map/ppermute | solution.py:56
  148.8 43.0 %collective-permute-start.21 = (bf16[640,512]{1,0:T(8,128)(2,1)S(1)}, bf16[640,512]{1,0:T(8,128)(2,1)S(1)}, u32[]{:S(2)}, u32[]{:S(2)}) collective-permute-start(bf16[640,512]{1,0:T(8,128)(2,1)S(1)} %collective-permute-done.20), channel_id=1, source_target_pairs={{0,4},{4,0},{8,12},{12,8},{16,20},{20,16},{24,28},{28,24},{1,5},{5... | collective-permute-start | bytes 1966088 | tf_op jit(solution)/shard_map/ppermute | solution.py:56
  150.6 45.3 %copy-start = (bf16[512,1024]{1,0:T(8,128)(2,1)S(1)}, bf16[512,1024]{1,0:T(8,128)(2,1)}, u32[]{:S(2)}) copy-start(bf16[512,1024]{1,0:T(8,128)(2,1)} %param.5) | copy-start | bytes 3145732
  150.7 42.2 %collective-permute-start.22 = (bf16[640,512]{1,0:T(8,128)(2,1)S(1)}, bf16[640,512]{1,0:T(8,128)(2,1)S(1)}, u32[]{:S(2)}, u32[]{:S(2)}) collective-permute-start(bf16[640,512]{1,0:T(8,128)(2,1)S(1)} %get-tuple-element.19), channel_id=1, source_target_pairs={{0,24},{4,28},{8,0},{12,4},{16,8},{20,12},{24,16},{28,20},{1,25},{... | collective-permute-start | bytes 1966088 | tf_op jit(solution)/shard_map/ppermute | solution.py:53
  191.8 32.6 %collective-permute-start.13 = (bf16[1024,640]{1,0:T(8,128)(2,1)S(1)}, bf16[1024,640]{1,0:T(8,128)(2,1)S(1)}, u32[]{:S(2)}, u32[]{:S(2)}) collective-permute-start(bf16[1024,640]{1,0:T(8,128)(2,1)S(1)} %pad_maximum_fusion.8), channel_id=1, source_target_pairs={{0,16},{4,20},{8,24},{12,28},{16,0},{20,4},{24,8},{28,12},{1,17},{... | collective-permute-start | bytes 3932168 | tf_op jit(solution)/shard_map/ppermute | solution.py:53
  192.9 57.5 %collective-permute-start.15 = (bf16[1024,640]{1,0:T(8,128)(2,1)S(1)}, bf16[1024,640]{1,0:T(8,128)(2,1)S(1)}, u32[]{:S(2)}, u32[]{:S(2)}) collective-permute-start(bf16[1024,640]{1,0:T(8,128)(2,1)S(1)} %pad_maximum_fusion.9), channel_id=1, source_target_pairs={{0,24},{4,28},{8,0},{12,4},{16,8},{20,12},{24,16},{28,20},{1,25},{... | collective-permute-start | bytes 3932168 | tf_op jit(solution)/shard_map/ppermute | solution.py:53
  194.4 17.6 %collective-permute-start.23 = (bf16[640,512]{1,0:T(8,128)(2,1)S(1)}, bf16[640,512]{1,0:T(8,128)(2,1)S(1)}, u32[]{:S(2)}, u32[]{:S(2)}) collective-permute-start(bf16[640,512]{1,0:T(8,128)(2,1)S(1)} %collective-permute-done.22), channel_id=1, source_target_pairs={{0,4},{4,0},{8,12},{12,8},{16,20},{20,16},{24,28},{28,24},{1,5},{5... | collective-permute-start | bytes 1966088 | tf_op jit(solution)/shard_map/ppermute | solution.py:56
  196.4 59.7 %collective-permute-start.12 = (bf16[1024,640]{1,0:T(8,128)(2,1)S(1)}, bf16[1024,640]{1,0:T(8,128)(2,1)S(1)}, u32[]{:S(2)}, u32[]{:S(2)}) collective-permute-start(bf16[1024,640]{1,0:T(8,128)(2,1)S(1)} %collective-permute-done.11), channel_id=1, source_target_pairs={{0,4},{4,0},{8,12},{12,8},{16,20},{20,16},{24,28},{28,24},{1,5},{5... | collective-permute-start | bytes 3932168 | tf_op jit(solution)/shard_map/ppermute | solution.py:56
  197.3 102.3 %collective-permute-start.6 = (bf16[2048,1024]{1,0:T(8,128)(2,1)S(1)}, bf16[2048,1024]{1,0:T(8,128)(2,1)}, u32[]{:S(2)}, u32[]{:S(2)}) collective-permute-start(bf16[2048,1024]{1,0:T(8,128)(2,1)S(1)} %pad_maximum_fusion.1), channel_id=1, source_target_pairs={{0,1},{1,0},{2,3},{3,2},{4,5},{5,4},{6,7},{7,6},{8,9},{9,8},{10,11... | collective-permute-start | bytes 12582920 | tf_op jit(solution)/shard_map/ppermute | solution.py:66
  212.0 87.6 %collective-permute-start.9 = (bf16[2048,1024]{1,0:T(8,128)(2,1)S(1)}, bf16[2048,1024]{1,0:T(8,128)(2,1)}, u32[]{:S(2)}, u32[]{:S(2)}) collective-permute-start(bf16[2048,1024]{1,0:T(8,128)(2,1)S(1)} %constant_dynamic-update-slice_fusion), channel_id=1, source_target_pairs={{0,1},{1,0},{2,3},{3,2},{4,5},{5,4},{6,7},{7,6},{8,9},{9,8},{10,11... | collective-permute-start | bytes 12582920 | tf_op jit(solution)/shard_map/ppermute | solution.py:66
  224.4 43.8 %collective-permute-start.14 = (bf16[1024,640]{1,0:T(8,128)(2,1)S(1)}, bf16[1024,640]{1,0:T(8,128)(2,1)S(1)}, u32[]{:S(2)}, u32[]{:S(2)}) collective-permute-start(bf16[1024,640]{1,0:T(8,128)(2,1)S(1)} %collective-permute-done.13), channel_id=1, source_target_pairs={{0,4},{4,0},{8,12},{12,8},{16,20},{20,16},{24,28},{28,24},{1,5},{5... | collective-permute-start | bytes 3932168 | tf_op jit(solution)/shard_map/ppermute | solution.py:56
  250.4 43.8 %collective-permute-start.16 = (bf16[1024,640]{1,0:T(8,128)(2,1)S(1)}, bf16[1024,640]{1,0:T(8,128)(2,1)S(1)}, u32[]{:S(2)}, u32[]{:S(2)}) collective-permute-start(bf16[1024,640]{1,0:T(8,128)(2,1)S(1)} %collective-permute-done.15), channel_id=1, source_target_pairs={{0,4},{4,0},{8,12},{12,8},{16,20},{20,16},{24,28},{28,24},{1,5},{5... | collective-permute-start | bytes 3932168 | tf_op jit(solution)/shard_map/ppermute | solution.py:56
  374.7 1.3 copy-start.3
  374.7 1.7 copy-start.4
  380.2 7.2 %collective-permute-start.32 = (bf16[1024,2048]{1,0:T(8,128)(2,1)S(1)}, bf16[1024,2048]{1,0:T(8,128)(2,1)S(1)}, u32[]{:S(2)}, u32[]{:S(2)}) collective-permute-start(bf16[1024,2048]{1,0:T(8,128)(2,1)S(1)} %convolution_convert_fusion), channel_id=1, source_target_pairs={{0,1},{1,0},{2,3},{3,2},{4,5},{5,4},{6,7},{7,6},{8,9},{9,8},{10,11... | collective-permute-start | bytes 12582920 | tf_op jit(solution)/shard_map/ppermute | solution.py:66
  384.3 9.1 %collective-permute-start.24 = (bf16[1024,2048]{1,0:T(8,128)(2,1)S(1)}, bf16[1024,2048]{1,0:T(8,128)(2,1)S(1)}, u32[]{:S(2)}, u32[]{:S(2)}) collective-permute-start(bf16[1024,2048]{1,0:T(8,128)(2,1)S(1)} %convolution_convert_fusion.1), channel_id=1, source_target_pairs={{0,1},{1,0},{2,3},{3,2},{4,5},{5,4},{6,7},{7,6},{8,9},{9,8},{10,11... | collective-permute-start | bytes 12582920 | tf_op jit(solution)/shard_map/ppermute | solution.py:66
  390.5 48.6 %collective-permute-start.33 = (bf16[1024,1024]{1,0:T(8,128)(2,1)S(1)}, bf16[1024,1024]{1,0:T(8,128)(2,1)S(1)}, u32[]{:S(2)}, u32[]{:S(2)}) collective-permute-start(bf16[1024,1024]{1,0:T(8,128)(2,1)S(1)} %add_convert_fusion.1), channel_id=1, source_target_pairs={{0,2},{1,3},{2,0},{3,1},{4,6},{5,7},{6,4},{7,5},{8,10},{9,11},{10,... | collective-permute-start | bytes 6291464 | tf_op jit(solution)/shard_map/ppermute | solution.py:61
  396.5 86.7 %collective-permute-start.25 = (bf16[1024,1024]{1,0:T(8,128)(2,1)S(1)}, bf16[1024,1024]{1,0:T(8,128)(2,1)S(1)}, u32[]{:S(2)}, u32[]{:S(2)}) collective-permute-start(bf16[1024,1024]{1,0:T(8,128)(2,1)S(1)} %add_convert_fusion.3), channel_id=1, source_target_pairs={{0,2},{1,3},{2,0},{3,1},{4,6},{5,7},{6,4},{7,5},{8,10},{9,11},{10,... | collective-permute-start | bytes 6291464 | tf_op jit(solution)/shard_map/ppermute | solution.py:61
  442.5 48.5 %collective-permute-start.34 = (bf16[256,1024]{1,0:T(8,128)(2,1)S(1)}, bf16[256,1024]{1,0:T(8,128)(2,1)S(1)}, u32[]{:S(2)}, u32[]{:S(2)}) collective-permute-start(bf16[256,1024]{1,0:T(8,128)(2,1)S(1)} %get-tuple-element.47), channel_id=1, source_target_pairs={{0,8},{4,12},{1,9},{5,13},{2,10},{6,14},{3,11},{7,15}} | collective-permute-start | bytes 1572872 | tf_op jit(solution)/shard_map/ppermute | solution.py:49
  446.1 44.8 %collective-permute-start.37 = (bf16[256,1024]{1,0:T(8,128)(2,1)S(1)}, bf16[256,1024]{1,0:T(8,128)(2,1)S(1)}, u32[]{:S(2)}, u32[]{:S(2)}) collective-permute-start(bf16[256,1024]{1,0:T(8,128)(2,1)S(1)} %get-tuple-element.48), channel_id=1, source_target_pairs={{24,16},{28,20},{25,17},{29,21},{26,18},{30,22},{27,19},{31,23}} | collective-permute-start | bytes 1572872 | tf_op jit(solution)/shard_map/ppermute | solution.py:49
  486.6 15.9 %collective-permute-start.26 = (bf16[256,1024]{1,0:T(8,128)(2,1)S(1)}, bf16[256,1024]{1,0:T(8,128)(2,1)S(1)}, u32[]{:S(2)}, u32[]{:S(2)}) collective-permute-start(bf16[256,1024]{1,0:T(8,128)(2,1)S(1)} %get-tuple-element.41), channel_id=1, source_target_pairs={{0,8},{4,12},{1,9},{5,13},{2,10},{6,14},{3,11},{7,15}} | collective-permute-start | bytes 1572872 | tf_op jit(solution)/shard_map/ppermute | solution.py:49
  490.3 12.3 %collective-permute-start.29 = (bf16[256,1024]{1,0:T(8,128)(2,1)S(1)}, bf16[256,1024]{1,0:T(8,128)(2,1)S(1)}, u32[]{:S(2)}, u32[]{:S(2)}) collective-permute-start(bf16[256,1024]{1,0:T(8,128)(2,1)S(1)} %get-tuple-element.42), channel_id=1, source_target_pairs={{24,16},{28,20},{25,17},{29,21},{26,18},{30,22},{27,19},{31,23}} | collective-permute-start | bytes 1572872 | tf_op jit(solution)/shard_map/ppermute | solution.py:49
  491.3 22.5 %collective-permute-start.35 = (bf16[256,1024]{1,0:T(8,128)(2,1)S(1)}, bf16[256,1024]{1,0:T(8,128)(2,1)S(1)}, u32[]{:S(2)}, u32[]{:S(2)}) collective-permute-start(bf16[256,1024]{1,0:T(8,128)(2,1)S(1)} %get-tuple-element.45), channel_id=1, source_target_pairs={{0,8},{4,12},{8,16},{12,20},{1,9},{5,13},{9,17},{13,21},{2,10},{6,... | collective-permute-start | bytes 1572872 | tf_op jit(solution)/shard_map/ppermute | solution.py:49
  492.6 21.1 %collective-permute-start.38 = (bf16[256,1024]{1,0:T(8,128)(2,1)S(1)}, bf16[256,1024]{1,0:T(8,128)(2,1)S(1)}, u32[]{:S(2)}, u32[]{:S(2)}) collective-permute-start(bf16[256,1024]{1,0:T(8,128)(2,1)S(1)} %get-tuple-element.46), channel_id=1, source_target_pairs={{16,8},{20,12},{24,16},{28,20},{17,9},{21,13},{25,17},{29,21},{18,... | collective-permute-start | bytes 1572872 | tf_op jit(solution)/shard_map/ppermute | solution.py:49
  502.8 22.1 %collective-permute-start.27 = (bf16[256,1024]{1,0:T(8,128)(2,1)S(1)}, bf16[256,1024]{1,0:T(8,128)(2,1)S(1)}, u32[]{:S(2)}, u32[]{:S(2)}) collective-permute-start(bf16[256,1024]{1,0:T(8,128)(2,1)S(1)} %get-tuple-element.39), channel_id=1, source_target_pairs={{0,8},{4,12},{8,16},{12,20},{1,9},{5,13},{9,17},{13,21},{2,10},{6,... | collective-permute-start | bytes 1572872 | tf_op jit(solution)/shard_map/ppermute | solution.py:49
  507.3 17.7 %collective-permute-start.30 = (bf16[256,1024]{1,0:T(8,128)(2,1)S(1)}, bf16[256,1024]{1,0:T(8,128)(2,1)S(1)}, u32[]{:S(2)}, u32[]{:S(2)}) collective-permute-start(bf16[256,1024]{1,0:T(8,128)(2,1)S(1)} %get-tuple-element.40), channel_id=1, source_target_pairs={{16,8},{20,12},{24,16},{28,20},{17,9},{21,13},{25,17},{29,21},{18,... | collective-permute-start | bytes 1572872 | tf_op jit(solution)/shard_map/ppermute | solution.py:49
  514.2 17.6 %collective-permute-start.39 = (bf16[256,1024]{1,0:T(8,128)(2,1)S(1)}, bf16[256,1024]{1,0:T(8,128)(2,1)S(1)}, u32[]{:S(2)}, u32[]{:S(2)}) collective-permute-start(bf16[256,1024]{1,0:T(8,128)(2,1)S(1)} %get-tuple-element.44), channel_id=1, source_target_pairs={{8,0},{12,4},{16,8},{20,12},{24,16},{28,20},{9,1},{13,5},{17,9},{2... | collective-permute-start | bytes 1572872 | tf_op jit(solution)/shard_map/ppermute | solution.py:49
  515.5 20.8 %collective-permute-start.36 = (bf16[256,1024]{1,0:T(8,128)(2,1)S(1)}, bf16[256,1024]{1,0:T(8,128)(2,1)S(1)}, u32[]{:S(2)}, u32[]{:S(2)}) collective-permute-start(bf16[256,1024]{1,0:T(8,128)(2,1)S(1)} %get-tuple-element.43), channel_id=1, source_target_pairs={{0,8},{4,12},{8,16},{12,20},{16,24},{20,28},{1,9},{5,13},{9,17},{1... | collective-permute-start | bytes 1572872 | tf_op jit(solution)/shard_map/ppermute | solution.py:49
  525.4 13.2 %collective-permute-start.31 = (bf16[256,1024]{1,0:T(8,128)(2,1)S(1)}, bf16[256,1024]{1,0:T(8,128)(2,1)S(1)}, u32[]{:S(2)}, u32[]{:S(2)}) collective-permute-start(bf16[256,1024]{1,0:T(8,128)(2,1)S(1)} %get-tuple-element.38), channel_id=1, source_target_pairs={{8,0},{12,4},{16,8},{20,12},{24,16},{28,20},{9,1},{13,5},{17,9},{2... | collective-permute-start | bytes 1572872 | tf_op jit(solution)/shard_map/ppermute | solution.py:49
  526.7 19.1 %collective-permute-start.28 = (bf16[256,1024]{1,0:T(8,128)(2,1)S(1)}, bf16[256,1024]{1,0:T(8,128)(2,1)S(1)}, u32[]{:S(2)}, u32[]{:S(2)}) collective-permute-start(bf16[256,1024]{1,0:T(8,128)(2,1)S(1)} %get-tuple-element.37), channel_id=1, source_target_pairs={{0,8},{4,12},{8,16},{12,20},{16,24},{20,28},{1,9},{5,13},{9,17},{1... | collective-permute-start | bytes 1572872 | tf_op jit(solution)/shard_map/ppermute | solution.py:49
